TPU v7x, 32 devices: a whole 2x2x4 slice. The times are simulated.
32 devices in a mesh: leaf: 8 (over z, x), cols: 4 (over y, core).
Axes of the slice: x: 2, y: 2, z: 4, core: 2. Of those that a mesh axis runs over, the one named last changes fastest.
Arguments:
- samples: bfloat16 [2048, 16384], P('cols', 'leaf'), may hold values from -6 to 6
- order_perm: int32 [16384], P('leaf'), may hold values from 0 to 16383, as said below
- leaf_factor: bfloat16 [16, 1024, 1024], P('leaf'), may hold values from -0.1875 to 0.1875
- bases: bfloat16 [4, 64, 16384], P(None, None, 'leaf'), may hold values from -110 to 110
- coupling: float32 [4, 8, 64, 64], P(None, 'leaf'), may hold values from -1 to 1, as said below
- ranks: int32 [4, 16], replicated, may hold values from 16 to 64
Outputs:
- transformed: float32 [2048, 16384], P('cols', 'leaf')
Inputs may be any that keep to these rules, and one draw needn't show every extreme that they name: `order_perm`: each aligned block of 2048 positions holds a permutation of the same block's indices. coupling[l, d] equals coupling[l, e] whenever d and e lie in the same level-l node, that is d // 2**l == e // 2**l.
All inputs are finite; a program needn't handle non-finite values.
Results may differ from a plain program's by a relative error of at most 0.0003.
Values sent between devices are 32-bit elements; how exact they have to be, the bound alone decides.
A program may use at most 128 MiB of HBM per device.

v0:
```python
import functools
import math

import jax
import jax.numpy as jnp
from jax import lax
from jax.experimental import pallas as pl
from jax.experimental.pallas import tpu as pltpu
from jax.sharding import PartitionSpec as P

HIGH = lax.Precision.HIGHEST
MIB = 1024 * 1024
BLOCK = 256


def dot_high(a, b, contract=((1,), (0,))):
    return lax.dot_general(
        a, b, (contract, ((), ())), precision=HIGH, preferred_element_type=jnp.float32
    )


def dot_bf16(a, b, contract=((1,), (0,))):
    return lax.dot_general(a, b, (contract, ((), ())), preferred_element_type=jnp.float32)


def split(values):
    high = values.astype(jnp.bfloat16)
    return high, (values - high.astype(jnp.float32)).astype(jnp.bfloat16)


def mask(rank_value, rank_width, scale, axis):
    shape = (1, rank_width) if axis else (rank_width, 1)
    return jnp.where(lax.broadcasted_iota(jnp.int32, shape, axis) < rank_value, scale, 0.0)


def place_system(table, slot, link, gram):
    width = link.shape[0]
    rows = lax.broadcasted_iota(jnp.int32, (width, width), 0)
    eye = (rows == lax.broadcasted_iota(jnp.int32, (width, width), 1)).astype(jnp.float32)
    system = eye + dot_high(dot_high(link, gram), link, ((1,), (1,)))
    table[slot, :, :width] = system
    table[slot, :, width:] = link


def eliminate(table, slots, pivot):
    width, span = table.shape[1:]
    lanes = lax.broadcasted_iota(jnp.int32, (width, span), 1)
    rows = lax.broadcasted_iota(jnp.int32, (width, span), 0)
    for slot in slots:
        now = table[slot]
        row = table[slot, pl.ds(pivot, 1), :]
        column = jnp.sum(jnp.where(lanes == pivot, now, 0.0), axis=1, keepdims=True)
        top = jnp.sum(jnp.where(lanes[:1] == pivot, row, 0.0), axis=1, keepdims=True)
        row = row / top
        table[slot] = jnp.where(rows == pivot, row, now - column * row)


def pair_order(levels):
    return [(l, m) for m in range(1, levels) for l in range(m, levels)]


def local_kernel(levels, width, ranks, samples, order, basis, coupling, leaf_hbm,
                 permuted, proj_out, first_out, gram_out, leaf, table, grams, weights, sem):
    device = lax.axis_index("leaf")
    row_count = samples.shape[1]
    half = row_count // 2
    fetch = pltpu.make_async_copy(leaf_hbm, leaf, sem)
    fetch.start()
    for side in range(2):
        part = basis[:, side * half:(side + 1) * half]
        grams[side] = dot_bf16(part, part, ((1,), (1,)))
    for index, (l, m) in enumerate(pair_order(levels)):
        rows, cols = pl.ds(l * width, width), pl.ds(m * width, width)
        gram_out[index // 2, :, pl.ds(index % 2 * width, width)] = (
            grams[0, rows, cols] + grams[1, rows, cols]
        )
    scale = 1.0 / math.sqrt(half)
    rank = [ranks[0, 2 * device], ranks[0, 2 * device + 1]]
    link = coupling[0, 0]
    links = [link, link.T]
    for side in range(2):
        scaled = links[side] * mask(rank[1 - side], width, scale, 1)
        place_system(table, side, scaled, grams[1 - side, :width, :width])

    blocks = row_count // BLOCK
    per_block = width // blocks

    def permute(block, carry):
        cols = pl.ds(pl.multiple_of(block * BLOCK, BLOCK), BLOCK)
        source = order[:, cols] - device * row_count
        picks = lax.broadcasted_iota(jnp.int32, (row_count, BLOCK), 0) == source
        picks = picks.astype(jnp.float32).astype(jnp.bfloat16)
        permuted[:, cols] = dot_bf16(samples[...], picks).astype(jnp.bfloat16)
        for step in range(per_block):
            eliminate(table, range(2), block * per_block + step)
        return carry

    lax.fori_loop(0, blocks, permute, 0)
    fetch.wait()
    height = levels * width
    projs = []
    for side in range(2):
        cols = slice(side * half, (side + 1) * half)
        high, low = split(dot_bf16(basis[:, cols], leaf[side], ((1,), (1,))))
        weights[:height] = high
        weights[height:] = low
        both = dot_bf16(weights[...], permuted[:, cols], ((1,), (1,)))
        projs.append(both[:height] + both[height:])
    later = projs[0][width:] + projs[1][width:]
    for side in range(2):
        solved = table[side, :, width:] * mask(rank[side], width, scale, 0)
        update = dot_high(solved, projs[1 - side][:width])
        first_out[side] = update
        later = later - dot_high(grams[side, width:, :width], update)
    chunks, _, chunk = proj_out.shape
    for index in range(chunks):
        proj_out[index] = later[:, index * chunk:(index + 1) * chunk]


def tree_kernel(levels, width, leaf_rows, ranks, grams, proj, coupling, update_out,
                gram_sum, gram_recv, proj_sum, proj_recv, table,
                gram_send_sem, gram_recv_sem, proj_send_sem, proj_recv_sem):
    device = lax.axis_index("leaf")
    steps = levels - 1
    chunks, _, chunk = proj.shape
    order = pair_order(levels)
    pairs = grams.shape[0]

    def partner(step):
        stride = 2 ** (step - 1)
        return device + stride * (1 - 2 * (device // stride % 2))

    barrier = pltpu.get_barrier_semaphore()
    for step in range(1, levels):
        pl.semaphore_signal(
            barrier, inc=1, device_id={"leaf": partner(step)},
            device_id_type=pl.DeviceIdType.MESH,
        )
    pl.semaphore_wait(barrier, steps)

    def gram_own(step):
        return grams if step == 1 else gram_sum.at[step - 2]

    def proj_own(step, index):
        return proj.at[index] if step == 1 else proj_sum.at[step - 2, index]

    def send_gram(step):
        first = order.index((step, step)) // 2
        kept = pl.ds(first, pairs - first)
        return pltpu.make_async_remote_copy(
            src_ref=gram_own(step).at[kept],
            dst_ref=gram_recv.at[step - 1, kept],
            send_sem=gram_send_sem.at[step - 1],
            recv_sem=gram_recv_sem.at[step - 1],
            device_id={"leaf": partner(step)},
            device_id_type=pl.DeviceIdType.MESH,
        )

    def send_proj(step, index):
        kept = pl.ds((step - 1) * width, (levels - step) * width)
        return pltpu.make_async_remote_copy(
            src_ref=proj_own(step, index).at[kept],
            dst_ref=proj_recv.at[step - 1, index, kept],
            send_sem=proj_send_sem.at[step - 1, index],
            recv_sem=proj_recv_sem.at[step - 1, index],
            device_id={"leaf": partner(step)},
            device_id_type=pl.DeviceIdType.MESH,
        )

    def block(ref, pair):
        index = order.index(pair)
        return ref[index // 2, :, pl.ds(index % 2 * width, width)]

    gram_copies = [send_gram(1)]
    gram_copies[0].start()
    proj_copies = {}
    for index in range(chunks):
        proj_copies[1, index] = send_proj(1, index)
        proj_copies[1, index].start()
    masks = {}
    for step in range(1, levels):
        gram_copies[step - 1].wait_recv()
        first = order.index((step, step)) // 2
        if step < steps:
            kept = pl.ds(first, pairs - first)
            gram_sum[step - 1, kept] = gram_own(step)[kept] + gram_recv[step - 1, kept]
            gram_copies.append(send_gram(step + 1))
            gram_copies[step].start()
        scale = 1.0 / math.sqrt(leaf_rows * 2 ** step)
        stride = 2 ** (step - 1)
        child = device // stride
        second = child % 2
        sibling = child + 1 - 2 * second
        rank_own = ranks[step, child * 2 ** step]
        rank_other = ranks[step, sibling * 2 ** step]
        masks[step] = (mask(rank_own, width, scale, 0), mask(rank_other, width, scale, 0))
        link = coupling[step, 0]
        link_own = jnp.where(second == 1, link.T, link)
        scaled = link_own * mask(rank_other, width, scale, 1)
        place_system(table, 2 * step - 2, scaled, block(gram_recv.at[step - 1], (step, step)))
        if step < steps:
            scaled = link_own.T * mask(rank_own, width, scale, 1)
            place_system(table, 2 * step - 1, scaled, block(gram_own(step), (step, step)))

    def pivot_step(pivot, carry):
        eliminate(table, range(2 * steps - 1), pivot)
        return carry

    lax.fori_loop(0, width, pivot_step, 0)

    for step in range(1, levels):
        base = (step - 1) * width
        solved_own = table[2 * step - 2, :, width:] * masks[step][0]
        if step < steps:
            solved_other = table[2 * step - 1, :, width:] * masks[step][1]
        for index in range(chunks):
            proj_copies[step, index].wait_recv()
            mine, other = proj_own(step, index), proj_recv.at[step - 1, index]
            update_own = dot_high(solved_own, other[pl.ds(base, width)])
            update_out[pl.ds(base, width), pl.ds(index * chunk, chunk)] = update_own
            if step == steps:
                continue
            update_other = dot_high(solved_other, mine[pl.ds(base, width)])
            for level in range(step + 1, levels):
                rows = pl.ds((level - 1) * width, width)
                new = mine[rows] + other[rows]
                new = new - dot_high(block(gram_own(step), (level, step)), update_own)
                new = new - dot_high(
                    block(gram_recv.at[step - 1], (level, step)), update_other
                )
                proj_sum[step - 1, index, rows] = new
            proj_copies[step + 1, index] = send_proj(step + 1, index)
            proj_copies[step + 1, index].start()
    for copy in gram_copies + list(proj_copies.values()):
        copy.wait_send()


def final_kernel(permuted, leaf, basis, first, later, out):
    update = jnp.concatenate([first[0], later[...]], axis=0)
    high, low = split(update)
    field = dot_bf16(permuted[...], leaf[0])
    field = field - dot_bf16(high, basis[...], ((0,), (0,)))
    out[...] = field - dot_bf16(low, basis[...], ((0,), (0,)))


def local(samples, order_perm, leaf_factor, bases, coupling, ranks):
    cols, row_count = samples.shape
    levels, width, _ = bases.shape
    leaf_rows = leaf_factor.shape[1]
    steps = levels - 1
    basis = bases.reshape(levels * width, row_count)
    pairs = (len(pair_order(levels)) + 1) // 2
    chunks = 2
    chunk = cols // chunks
    vmem = pl.BlockSpec(memory_space=pltpu.VMEM)
    smem = pl.BlockSpec(memory_space=pltpu.SMEM)
    f32 = jnp.float32
    permuted, proj, first, grams = pl.pallas_call(
        functools.partial(local_kernel, levels, width),
        name="local_part",
        out_shape=(
            jax.ShapeDtypeStruct((cols, row_count), jnp.bfloat16),
            jax.ShapeDtypeStruct((chunks, steps * width, chunk), f32),
            jax.ShapeDtypeStruct((2, width, cols), f32),
            jax.ShapeDtypeStruct((pairs, width, 2 * width), f32),
        ),
        in_specs=[smem, vmem, vmem, vmem, vmem, pl.BlockSpec(memory_space=pl.ANY)],
        out_specs=(vmem,) * 4,
        scratch_shapes=[
            pltpu.VMEM(leaf_factor.shape, jnp.bfloat16),
            pltpu.VMEM((2, width, 2 * width), f32),
            pltpu.VMEM((2, levels * width, levels * width), f32),
            pltpu.VMEM((2 * levels * width, leaf_rows), jnp.bfloat16),
            pltpu.SemaphoreType.DMA,
        ],
        compiler_params=pltpu.CompilerParams(vmem_limit_bytes=48 * MIB),
    )(ranks, samples, order_perm.reshape(1, row_count), basis, coupling, leaf_factor)
    later = pl.pallas_call(
        functools.partial(tree_kernel, levels, width, leaf_rows),
        name="tree_part",
        out_shape=jax.ShapeDtypeStruct((steps * width, cols), f32),
        in_specs=[smem, vmem, vmem, vmem],
        out_specs=vmem,
        scratch_shapes=[
            pltpu.VMEM((max(steps - 1, 1), pairs, width, 2 * width), f32),
            pltpu.VMEM((steps, pairs, width, 2 * width), f32),
            pltpu.VMEM((max(steps - 1, 1), chunks, steps * width, chunk), f32),
            pltpu.VMEM((steps, chunks, steps * width, chunk), f32),
            pltpu.VMEM((2 * steps - 1, width, 2 * width), f32),
            pltpu.SemaphoreType.DMA((steps,)),
            pltpu.SemaphoreType.DMA((steps,)),
            pltpu.SemaphoreType.DMA((steps, chunks)),
            pltpu.SemaphoreType.DMA((steps, chunks)),
        ],
        compiler_params=pltpu.CompilerParams(
            collective_id=0, has_side_effects=True, vmem_limit_bytes=48 * MIB
        ),
    )(ranks, grams, proj, coupling)
    tile = leaf_rows // 2
    per_leaf = leaf_rows // tile
    return pl.pallas_call(
        final_kernel,
        name="final_part",
        grid=(row_count // tile,),
        out_shape=jax.ShapeDtypeStruct((cols, row_count), f32),
        in_specs=[
            pl.BlockSpec((cols, leaf_rows), lambda j: (0, j // per_leaf)),
            pl.BlockSpec((1, leaf_rows, tile), lambda j: (j // per_leaf, 0, j % per_leaf)),
            pl.BlockSpec((levels * width, tile), lambda j: (0, j)),
            pl.BlockSpec((1, width, cols), lambda j: (j // per_leaf, 0, 0)),
            pl.BlockSpec((steps * width, cols), lambda j: (0, 0)),
        ],
        out_specs=pl.BlockSpec((cols, tile), lambda j: (0, j)),
        compiler_params=pltpu.CompilerParams(vmem_limit_bytes=48 * MIB),
    )(permuted, leaf_factor, basis, first, later)


def solution(mesh):
    in_specs = (
        P("cols", "leaf"),
        P("leaf"),
        P("leaf", None, None),
        P(None, None, "leaf"),
        P(None, "leaf", None, None),
        P(),
    )
    out_specs = P("cols", "leaf")
    return jax.shard_map(local, mesh=mesh, in_specs=in_specs, out_specs=out_specs, check_vma=False)
```

profile of v0, /device:TPU:0, one launch (start us, length us, event | category | flops | bytes accessed | tf_op | source)
XLA Modules:
  0.0 88.6 jit_solution(1250873029021761815)
XLA Ops:
  0.0 0.0 copy-start
  0.0 1.2 %copy-done = bf16[4,64,2048]{2,1,0:T(8,128)(2,1)S(1)} copy-done((bf16[4,64,2048]{2,1,0:T(8,128)(2,1)S(1)}, bf16[4,64,2048]{2,1,0:T(8,128)(2,1)}, u32[]{:S(2)}) %copy-start) | copy-done | bytes 1048600
  1.2 0.0 copy-start.2
  1.2 1.6 %copy-done.2 = bf16[512,2048]{1,0:T(8,128)(2,1)S(1)} copy-done((bf16[512,2048]{1,0:T(8,128)(2,1)S(1)}, bf16[512,2048]{1,0:T(8,128)(2,1)}, u32[]{:S(2)}) %copy-start.2) | copy-done | bytes 2097176
  2.8 0.0 copy-start.3
  2.8 0.9 %copy-done.3 = f32[4,1,64,64]{3,2,1,0:T(8,128)S(1)} copy-done((f32[4,1,64,64]{3,2,1,0:T(8,128)S(1)}, f32[4,1,64,64]{3,2,1,0:T(8,128)}, u32[]{:S(2)}) %copy-start.3) | copy-done | bytes 65560
  3.7 0.0 copy-start.4
  3.7 0.7 copy-done.4
  4.4 0.0 copy-start.5
  4.4 0.7 copy-done.5
  5.1 0.0 copy-start.1
  5.1 17.1 %local_part.1 = (bf16[512,2048]{1,0:T(8,128)(2,1)S(1)}, f32[2,192,256]{2,1,0:T(8,128)S(1)}, f32[2,64,512]{2,1,0:T(8,128)S(1)}, f32[3,64,128]{2,1,0:T(8,128)S(1)}) custom-call(s32[4,16]{1,0:T(4,128)S(1)} %copy-done.5, bf16[512,2048]{1,0:T(8,128)(2,1)S(1)} %copy-done.2, s32[1,2048]{1,0:T(1,128)S(1)} %bitcast.4, bf16[256,2048]{1,0:T(8,128)(2,1)S(1)} %bitcast.2, ...), custom_call_target="tpu_custom_call" | custom-call | tf_op jit(solution)/shard_map/local_part/pallas_call | solution.py:258
  22.2 59.2 %tree_part.1.later = f32[192,512]{1,0:T(8,128)S(1)} custom-call(s32[4,16]{1,0:T(4,128)S(1)} %copy-done.5, f32[3,64,128]{2,1,0:T(8,128)S(1)} %get-tuple-element.11.grams, f32[2,192,256]{2,1,0:T(8,128)S(1)} %get-tuple-element.12.proj, f32[4,1,64,64]{3,2,1,0:T(8,128)S(1)} %copy-done.3), custom_call_target="tpu_custom_call" | custom-call | tf_op jit(solution)/shard_map/tree_part/pallas_call | solution.py:278
  81.5 0.0 copy-done.1
  81.5 7.1 %final_part.1 = f32[512,2048]{1,0:T(8,128)} custom-call(bf16[512,2048]{1,0:T(8,128)(2,1)S(1)} %get-tuple-element.9.permuted, bf16[2,1024,1024]{2,1,0:T(8,128)(2,1)} %leaf.1, bf16[256,2048]{1,0:T(8,128)(2,1)S(1)} %bitcast.3, f32[2,64,512]{2,1,0:T(8,128)S(1)} %get-tuple-element.10.first, f32[192,512]{1,0:T(8,128)S(1)} %tree_part.1.later), custom_call_target="tpu_custom_call" | custom-call | tf_op jit(solution)/shard_map/final_part/pallas_call | solution.py:301
Async XLA Ops:
  0.0 1.2 %copy-start = (bf16[4,64,2048]{2,1,0:T(8,128)(2,1)S(1)}, bf16[4,64,2048]{2,1,0:T(8,128)(2,1)}, u32[]{:S(2)}) copy-start(bf16[4,64,2048]{2,1,0:T(8,128)(2,1)} %param.9) | copy-start | bytes 3145732
  1.2 1.6 %copy-start.2 = (bf16[512,2048]{1,0:T(8,128)(2,1)S(1)}, bf16[512,2048]{1,0:T(8,128)(2,1)}, u32[]{:S(2)}) copy-start(bf16[512,2048]{1,0:T(8,128)(2,1)} %samples.1) | copy-start | bytes 6291460
  2.8 0.9 %copy-start.3 = (f32[4,1,64,64]{3,2,1,0:T(8,128)S(1)}, f32[4,1,64,64]{3,2,1,0:T(8,128)}, u32[]{:S(2)}) copy-start(f32[4,1,64,64]{3,2,1,0:T(8,128)} %coupling.3) | copy-start | bytes 196612
  3.7 0.7 copy-start.4
  4.4 0.7 copy-start.5
  5.1 76.4 %copy-start.1 = (bf16[4,64,2048]{2,1,0:T(8,128)(2,1)S(1)}, bf16[4,64,2048]{2,1,0:T(8,128)(2,1)}, u32[]{:S(2)}) copy-start(bf16[4,64,2048]{2,1,0:T(8,128)(2,1)} %param.9) | copy-start | bytes 3145732
where the time goes:
time: 89 us; the launch traced here: 88.6 us
  Pallas kernels  83.5 us (94%)
  local copies, waits for them, and re-layouts  5.1 us (6%)
    pallas_call x1, Pallas kernels, local(): pl.pallas_call(functools.partial(tree_kernel, levels, width, leaf_rows),...  59.2 us
    pallas_call x1, Pallas kernels, local(): pl.pallas_call(functools.partial(local_kernel, levels, width), name='loca...  17.1 us
    pallas_call x1, Pallas kernels, local(): pl.pallas_call(final_kernel, name='final_part', grid=(row_count // tile,)...  7.13 us
    unnamed x12, local copies, waits for them, and re-layouts  5.1 us

commit v1 on v0

v1 whole, which is shorter than its diff:
```python
import functools
import math

import jax
import jax.numpy as jnp
from jax import lax
from jax.experimental import pallas as pl
from jax.experimental.pallas import tpu as pltpu
from jax.sharding import PartitionSpec as P

HIGH = lax.Precision.HIGHEST
MIB = 1024 * 1024
BLOCK = 256
PIVOTS = 8


def dot_high(a, b, contract=((1,), (0,))):
    return lax.dot_general(
        a, b, (contract, ((), ())), precision=HIGH, preferred_element_type=jnp.float32
    )


def dot_bf16(a, b, contract=((1,), (0,))):
    return lax.dot_general(a, b, (contract, ((), ())), preferred_element_type=jnp.float32)


def split(values):
    high = values.astype(jnp.bfloat16)
    return high, (values - high.astype(jnp.float32)).astype(jnp.bfloat16)


def mask(rank_value, rank_width, scale, axis):
    shape = (1, rank_width) if axis else (rank_width, 1)
    return jnp.where(lax.broadcasted_iota(jnp.int32, shape, axis) < rank_value, scale, 0.0)


def place_system(table, slot, link, gram):
    width = link.shape[0]
    rows = lax.broadcasted_iota(jnp.int32, (width, width), 0)
    eye = (rows == lax.broadcasted_iota(jnp.int32, (width, width), 1)).astype(jnp.float32)
    system = eye + dot_high(dot_high(link, gram), link, ((1,), (1,)))
    table[slot, :, :width] = system
    table[slot, :, width:] = link


def eliminate(table, slots, block):
    width, span = table.shape[1:]
    rows = lax.broadcasted_iota(jnp.int32, (PIVOTS, span), 0)
    place = pl.ds(pl.multiple_of(block * PIVOTS, PIVOTS), PIVOTS)
    whole = [table[slot] for slot in slots]
    panels = [table[slot, place, :] for slot in slots]
    for pivot in range(PIVOTS):
        for index, panel in enumerate(panels):
            column = panel[:, pivot:pivot + 1]
            row = panel[pivot:pivot + 1, :] * (1.0 / column[pivot:pivot + 1])
            panels[index] = jnp.where(rows == pivot, row, panel - column * row)
    new = [now - dot_high(now[:, :PIVOTS], panel) for now, panel in zip(whole, panels)]
    for slot, now, panel in zip(slots, new, panels):
        table[slot] = pltpu.roll(now, span - PIVOTS, 1)
        table[slot, place, :] = pltpu.roll(panel, span - PIVOTS, 1)


def pair_order(levels):
    return [(l, m) for m in range(1, levels) for l in range(m, levels)]


def tree_kernel(levels, width, ranks, samples_hbm, order_hbm, basis_hbm, coupling_hbm, leaf_hbm,
                permuted, first_out, update_out,
                samples, order, basis, coupling, leaf, local_grams, weights, first_table,
                gram_first, gram_sum, gram_recv, proj_first, proj_sum, proj_recv, table,
                fetch_sem, gram_send_sem, gram_recv_sem, proj_send_sem, proj_recv_sem):
    device = lax.axis_index("leaf")
    steps = levels - 1
    chunks, _, chunk = proj_first.shape
    pair_list = pair_order(levels)
    pairs = gram_first.shape[0]
    row_count = samples.shape[1]
    half = row_count // 2
    height = levels * width

    fetches = [
        pltpu.make_async_copy(source, target, fetch_sem.at[index])
        for index, (source, target) in enumerate((
            (basis_hbm, basis), (coupling_hbm, coupling), (order_hbm, order),
            (samples_hbm, samples), (leaf_hbm, leaf),
        ))
    ]
    for fetch in fetches:
        fetch.start()

    def partner(step):
        stride = 2 ** (step - 1)
        return device + stride * (1 - 2 * (device // stride % 2))

    barrier = pltpu.get_barrier_semaphore()
    for step in range(1, levels):
        pl.semaphore_signal(
            barrier, inc=1, device_id={"leaf": partner(step)},
            device_id_type=pl.DeviceIdType.MESH,
        )

    def gram_own(step):
        return gram_first if step == 1 else gram_sum.at[step - 2]

    def proj_own(step, index):
        return proj_first.at[index] if step == 1 else proj_sum.at[step - 2, index]

    def send_gram(step):
        first = pair_list.index((step, step)) // 2
        kept = pl.ds(first, pairs - first)
        return pltpu.make_async_remote_copy(
            src_ref=gram_own(step).at[kept],
            dst_ref=gram_recv.at[step - 1, kept],
            send_sem=gram_send_sem.at[step - 1],
            recv_sem=gram_recv_sem.at[step - 1],
            device_id={"leaf": partner(step)},
            device_id_type=pl.DeviceIdType.MESH,
        )

    def send_proj(step, index):
        kept = pl.ds((step - 1) * width, (levels - step) * width)
        return pltpu.make_async_remote_copy(
            src_ref=proj_own(step, index).at[kept],
            dst_ref=proj_recv.at[step - 1, index, kept],
            send_sem=proj_send_sem.at[step - 1, index],
            recv_sem=proj_recv_sem.at[step - 1, index],
            device_id={"leaf": partner(step)},
            device_id_type=pl.DeviceIdType.MESH,
        )

    def block(ref, pair):
        index = pair_list.index(pair)
        return ref[index // 2, :, pl.ds(index % 2 * width, width)]

    fetches[0].wait()
    for side in range(2):
        part = basis[:, side * half:(side + 1) * half]
        local_grams[side] = dot_bf16(part, part, ((1,), (1,)))
    for index, (l, m) in enumerate(pair_list):
        rows, cols = pl.ds(l * width, width), pl.ds(m * width, width)
        gram_first[index // 2, :, pl.ds(index % 2 * width, width)] = (
            local_grams[0, rows, cols] + local_grams[1, rows, cols]
        )
    if len(pair_list) % 2:
        gram_first[pairs - 1, :, pl.ds(width, width)] = jnp.zeros((width, width), jnp.float32)
    pl.semaphore_wait(barrier, steps)
    gram_copies = [send_gram(1)]
    gram_copies[0].start()

    scale = 1.0 / math.sqrt(half)
    rank = [ranks[0, 2 * device], ranks[0, 2 * device + 1]]
    fetches[1].wait()
    link = coupling[0, 0]
    links = [link, link.T]
    for side in range(2):
        scaled = links[side] * mask(rank[1 - side], width, scale, 1)
        place_system(first_table, side, scaled, local_grams[1 - side, :width, :width])

    blocks = row_count // BLOCK
    per_block = width // PIVOTS // blocks

    def permute(now, carry):
        cols = pl.ds(pl.multiple_of(now * BLOCK, BLOCK), BLOCK)
        source = order[:, cols] - device * row_count
        picks = lax.broadcasted_iota(jnp.int32, (row_count, BLOCK), 0) == source
        picks = picks.astype(jnp.float32).astype(jnp.bfloat16)
        permuted[:, cols] = dot_bf16(samples[...], picks).astype(jnp.bfloat16)
        for step in range(per_block):
            eliminate(first_table, range(2), now * per_block + step)
        return carry

    fetches[2].wait()
    fetches[3].wait()
    masks = {}
    for step in range(1, levels):
        lax.fori_loop(blocks * (step - 1) // steps, blocks * step // steps, permute, 0)
        gram_copies[step - 1].wait_recv()
        first = pair_list.index((step, step)) // 2
        if step < steps:
            kept = pl.ds(first, pairs - first)
            gram_sum[step - 1, kept] = gram_own(step)[kept] + gram_recv[step - 1, kept]
            gram_copies.append(send_gram(step + 1))
            gram_copies[step].start()
        scale = 1.0 / math.sqrt(half * 2 ** step)
        stride = 2 ** (step - 1)
        child = device // stride
        second = child % 2
        sibling = child + 1 - 2 * second
        rank_own = ranks[step, child * 2 ** step]
        rank_other = ranks[step, sibling * 2 ** step]
        masks[step] = (mask(rank_own, width, scale, 0), mask(rank_other, width, scale, 0))
        link = coupling[step, 0]
        link_own = jnp.where(second == 1, link.T, link)
        scaled = link_own * mask(rank_other, width, scale, 1)
        place_system(table, 2 * step - 2, scaled, block(gram_recv.at[step - 1], (step, step)))
        if step < steps:
            scaled = link_own.T * mask(rank_own, width, scale, 1)
            place_system(table, 2 * step - 1, scaled, block(gram_own(step), (step, step)))

    fetches[4].wait()
    projs = []
    for side in range(2):
        cols = slice(side * half, (side + 1) * half)
        high, low = split(dot_bf16(basis[:, cols], leaf[side], ((1,), (1,))))
        weights[:height] = high
        weights[height:] = low
        both = dot_bf16(weights[...], permuted[:, cols], ((1,), (1,)))
        projs.append(both[:height] + both[height:])
    later = projs[0][width:] + projs[1][width:]
    scale = 1.0 / math.sqrt(half)
    for side in range(2):
        solved = first_table[side, :, :width] * mask(rank[side], width, scale, 0)
        update = dot_high(solved, projs[1 - side][:width])
        first_out[side] = update
        later = later - dot_high(local_grams[side, width:, :width], update)
    proj_copies = {}
    for index in range(chunks):
        proj_first[index] = later[:, index * chunk:(index + 1) * chunk]
        proj_copies[1, index] = send_proj(1, index)
        proj_copies[1, index].start()

    def pivot_step(pivot, carry):
        eliminate(table, range(2 * steps - 1), pivot)
        return carry

    lax.fori_loop(0, width // PIVOTS, pivot_step, 0)

    for step in range(1, levels):
        base = (step - 1) * width
        solved_own = table[2 * step - 2, :, :width] * masks[step][0]
        if step < steps:
            solved_other = table[2 * step - 1, :, :width] * masks[step][1]
        for index in range(chunks):
            proj_copies[step, index].wait_recv()
            mine, other = proj_own(step, index), proj_recv.at[step - 1, index]
            update_own = dot_high(solved_own, other[pl.ds(base, width)])
            update_out[pl.ds(base, width), pl.ds(index * chunk, chunk)] = update_own
            if step == steps:
                continue
            update_other = dot_high(solved_other, mine[pl.ds(base, width)])
            for level in range(step + 1, levels):
                rows = pl.ds((level - 1) * width, width)
                new = mine[rows] + other[rows]
                new = new - dot_high(block(gram_own(step), (level, step)), update_own)
                new = new - dot_high(
                    block(gram_recv.at[step - 1], (level, step)), update_other
                )
                proj_sum[step - 1, index, rows] = new
            proj_copies[step + 1, index] = send_proj(step + 1, index)
            proj_copies[step + 1, index].start()
    for copy in gram_copies + list(proj_copies.values()):
        copy.wait_send()


def final_kernel(permuted, leaf, basis, first, later, out):
    update = jnp.concatenate([first[0], later[...]], axis=0)
    high, low = split(update)
    field = dot_bf16(permuted[...], leaf[0])
    field = field - dot_bf16(high, basis[...], ((0,), (0,)))
    out[...] = field - dot_bf16(low, basis[...], ((0,), (0,)))


def local(samples, order_perm, leaf_factor, bases, coupling, ranks):
    cols, row_count = samples.shape
    levels, width, _ = bases.shape
    leaf_rows = leaf_factor.shape[1]
    steps = levels - 1
    basis = bases.reshape(levels * width, row_count)
    pairs = (len(pair_order(levels)) + 1) // 2
    chunks = 4
    chunk = cols // chunks
    vmem = pl.BlockSpec(memory_space=pltpu.VMEM)
    smem = pl.BlockSpec(memory_space=pltpu.SMEM)
    f32 = jnp.float32
    hbm = pl.BlockSpec(memory_space=pltpu.MemorySpace.HBM)
    permuted, first, later = pl.pallas_call(
        functools.partial(tree_kernel, levels, width),
        name="tree_part",
        out_shape=(
            jax.ShapeDtypeStruct((cols, row_count), jnp.bfloat16),
            jax.ShapeDtypeStruct((2, width, cols), f32),
            jax.ShapeDtypeStruct((steps * width, cols), f32),
        ),
        in_specs=[smem, hbm, hbm, hbm, hbm, hbm],
        out_specs=(vmem,) * 3,
        scratch_shapes=[
            pltpu.VMEM(samples.shape, jnp.bfloat16),
            pltpu.VMEM((1, row_count), jnp.int32),
            pltpu.VMEM(basis.shape, jnp.bfloat16),
            pltpu.VMEM(coupling.shape, f32),
            pltpu.VMEM(leaf_factor.shape, jnp.bfloat16),
            pltpu.VMEM((2, levels * width, levels * width), f32),
            pltpu.VMEM((2 * levels * width, leaf_rows), jnp.bfloat16),
            pltpu.VMEM((2, width, 2 * width), f32),
            pltpu.VMEM((pairs, width, 2 * width), f32),
            pltpu.VMEM((max(steps - 1, 1), pairs, width, 2 * width), f32),
            pltpu.VMEM((steps, pairs, width, 2 * width), f32),
            pltpu.VMEM((chunks, steps * width, chunk), f32),
            pltpu.VMEM((max(steps - 1, 1), chunks, steps * width, chunk), f32),
            pltpu.VMEM((steps, chunks, steps * width, chunk), f32),
            pltpu.VMEM((2 * steps - 1, width, 2 * width), f32),
            pltpu.SemaphoreType.DMA((5,)),
            pltpu.SemaphoreType.DMA((steps,)),
            pltpu.SemaphoreType.DMA((steps,)),
            pltpu.SemaphoreType.DMA((steps, chunks)),
            pltpu.SemaphoreType.DMA((steps, chunks)),
        ],
        compiler_params=pltpu.CompilerParams(
            collective_id=0, has_side_effects=True, vmem_limit_bytes=63 * MIB
        ),
    )(ranks, samples, order_perm.reshape(1, row_count), basis, coupling, leaf_factor)
    tile = leaf_rows // 2
    per_leaf = leaf_rows // tile
    return pl.pallas_call(
        final_kernel,
        name="final_part",
        grid=(row_count // tile,),
        out_shape=jax.ShapeDtypeStruct((cols, row_count), f32),
        in_specs=[
            pl.BlockSpec((cols, leaf_rows), lambda j: (0, j // per_leaf)),
            pl.BlockSpec((1, leaf_rows, tile), lambda j: (j // per_leaf, 0, j % per_leaf)),
            pl.BlockSpec((levels * width, tile), lambda j: (0, j)),
            pl.BlockSpec((1, width, cols), lambda j: (j // per_leaf, 0, 0)),
            pl.BlockSpec((steps * width, cols), lambda j: (0, 0)),
        ],
        out_specs=pl.BlockSpec((cols, tile), lambda j: (0, j)),
        compiler_params=pltpu.CompilerParams(vmem_limit_bytes=63 * MIB),
    )(permuted, leaf_factor, basis, first, later)


def solution(mesh):
    in_specs = (
        P("cols", "leaf"),
        P("leaf"),
        P("leaf", None, None),
        P(None, None, "leaf"),
        P(None, "leaf", None, None),
        P(),
    )
    out_specs = P("cols", "leaf")
    return jax.shard_map(local, mesh=mesh, in_specs=in_specs, out_specs=out_specs, check_vma=False)
```

time: 89 us -> 51.5 us (0.58)
  Pallas kernels: 83.5 us -> 51.4 us
  local copies, waits for them, and re-layouts: 5.1 us -> 0 us
    pallas_call x2 -> x1, Pallas kernels: 76.4 us -> 43 us  [local(): pl.pallas_call(functools.partial(tree_kernel, levels, width), name='tree_...]
    unnamed x12 -> x0, local copies, waits for them, and re-layouts: 5.1 us -> none
    pallas_call x1, Pallas kernels: 7.13 us -> 8.32 us  [local(): pl.pallas_call(final_kernel, name='final_part', grid=(row_count // tile,)...]
where the time goes in v1:
time: 51.5 us; the launch traced here: 51.4 us
  Pallas kernels  51.4 us (100%)
    pallas_call x1, Pallas kernels, local(): pl.pallas_call(functools.partial(tree_kernel, levels, width), name='tree_...  43 us
    pallas_call x1, Pallas kernels, local(): pl.pallas_call(final_kernel, name='final_part', grid=(row_count // tile,)...  8.32 us

profile of v1, /device:TPU:0, one launch (start us, length us, event | category | flops | bytes accessed | tf_op | source)
XLA Modules:
  0.0 51.4 jit_solution(8570872680228651140)
XLA Ops:
  0.0 43.0 %tree_part.1 = (bf16[512,2048]{1,0:T(8,128)(2,1)}, f32[2,64,512]{2,1,0:T(8,128)}, f32[192,512]{1,0:T(8,128)}) custom-call(s32[4,16]{1,0:T(4,128)} %ranks.1, bf16[512,2048]{1,0:T(8,128)(2,1)} %samples_hbm.1, s32[1,2048]{1,0:T(1,128)} %bitcast.4, bf16[256,2048]{1,0:T(8,128)(2,1)} %bitcast.2, f32[4,1,64,64]{3,2,1,0:T(8,128)} %coupling_hbm.1, ...), custom_call_target="tpu_custom_call" | custom-call | tf_op jit(solution)/shard_map/tree_part/pallas_call | solution.py:276
  43.0 8.3 %final_part.1 = f32[512,2048]{1,0:T(8,128)} custom-call(bf16[512,2048]{1,0:T(8,128)(2,1)} %get-tuple-element.8.permuted, bf16[2,1024,1024]{2,1,0:T(8,128)(2,1)} %leaf.1, bf16[256,2048]{1,0:T(8,128)(2,1)} %bitcast.3, f32[2,64,512]{2,1,0:T(8,128)} %get-tuple-element.9.first, f32[192,512]{1,0:T(8,128)} %get-tuple-element.10.later), custom_call_target="tpu_custom_call" | custom-call | tf_op jit(solution)/shard_map/final_part/pallas_call | solution.py:314

commit v2 on v1

--- a/solution.py
+++ b/solution.py
@@ -65,10 +65,10 @@
 
 
 def tree_kernel(levels, width, ranks, samples_hbm, order_hbm, basis_hbm, coupling_hbm, leaf_hbm,
-                permuted, first_out, update_out,
-                samples, order, basis, coupling, leaf, local_grams, weights, first_table,
+                field_hbm, first_out, update_out,
+                field, permuted, samples, order, basis, coupling, leaf, local_grams, weights, first_table,
                 gram_first, gram_sum, gram_recv, proj_first, proj_sum, proj_recv, table,
-                fetch_sem, gram_send_sem, gram_recv_sem, proj_send_sem, proj_recv_sem):
+                fetch_sem, field_sem, gram_send_sem, gram_recv_sem, proj_send_sem, proj_recv_sem):
     device = lax.axis_index("leaf")
     steps = levels - 1
     chunks, _, chunk = proj_first.shape
@@ -220,10 +220,19 @@
         proj_copies[1, index].start()
 
     def pivot_step(pivot, carry):
+        side, place = pivot // (turns // 2), pivot % (turns // 2)
+        rows = pl.ds(pl.multiple_of(side * half, half), half)
+        cols = pl.ds(pl.multiple_of(place * tile, tile), tile)
+        target = pl.ds(pl.multiple_of(pivot * tile, tile), tile)
+        field[:, target] = dot_bf16(permuted[:, rows], leaf[side, :, cols])
         eliminate(table, range(2 * steps - 1), pivot)
         return carry
 
-    lax.fori_loop(0, width // PIVOTS, pivot_step, 0)
+    turns = width // PIVOTS
+    tile = row_count // turns
+    lax.fori_loop(0, turns, pivot_step, 0)
+    field_copy = pltpu.make_async_copy(field, field_hbm, field_sem)
+    field_copy.start()
 
     for step in range(1, levels):
         base = (step - 1) * width
@@ -250,14 +259,14 @@
             proj_copies[step + 1, index].start()
     for copy in gram_copies + list(proj_copies.values()):
         copy.wait_send()
-
-
-def final_kernel(permuted, leaf, basis, first, later, out):
+    field_copy.wait()
+
+
+def final_kernel(field, basis, first, later, out):
     update = jnp.concatenate([first[0], later[...]], axis=0)
     high, low = split(update)
-    field = dot_bf16(permuted[...], leaf[0])
-    field = field - dot_bf16(high, basis[...], ((0,), (0,)))
-    out[...] = field - dot_bf16(low, basis[...], ((0,), (0,)))
+    both = dot_bf16(high, basis[...], ((0,), (0,))) + dot_bf16(low, basis[...], ((0,), (0,)))
+    out[...] = field[...] - both
 
 
 def local(samples, order_perm, leaf_factor, bases, coupling, ranks):
@@ -273,17 +282,19 @@
     smem = pl.BlockSpec(memory_space=pltpu.SMEM)
     f32 = jnp.float32
     hbm = pl.BlockSpec(memory_space=pltpu.MemorySpace.HBM)
-    permuted, first, later = pl.pallas_call(
+    field, first, later = pl.pallas_call(
         functools.partial(tree_kernel, levels, width),
         name="tree_part",
         out_shape=(
-            jax.ShapeDtypeStruct((cols, row_count), jnp.bfloat16),
+            jax.ShapeDtypeStruct((cols, row_count), f32),
             jax.ShapeDtypeStruct((2, width, cols), f32),
             jax.ShapeDtypeStruct((steps * width, cols), f32),
         ),
         in_specs=[smem, hbm, hbm, hbm, hbm, hbm],
-        out_specs=(vmem,) * 3,
+        out_specs=(hbm, vmem, vmem),
         scratch_shapes=[
+            pltpu.VMEM(samples.shape, f32),
+            pltpu.VMEM(samples.shape, jnp.bfloat16),
             pltpu.VMEM(samples.shape, jnp.bfloat16),
             pltpu.VMEM((1, row_count), jnp.int32),
             pltpu.VMEM(basis.shape, jnp.bfloat16),
@@ -300,6 +311,7 @@
             pltpu.VMEM((steps, chunks, steps * width, chunk), f32),
             pltpu.VMEM((2 * steps - 1, width, 2 * width), f32),
             pltpu.SemaphoreType.DMA((5,)),
+            pltpu.SemaphoreType.DMA,
             pltpu.SemaphoreType.DMA((steps,)),
             pltpu.SemaphoreType.DMA((steps,)),
             pltpu.SemaphoreType.DMA((steps, chunks)),
@@ -317,15 +329,14 @@
         grid=(row_count // tile,),
         out_shape=jax.ShapeDtypeStruct((cols, row_count), f32),
         in_specs=[
-            pl.BlockSpec((cols, leaf_rows), lambda j: (0, j // per_leaf)),
-            pl.BlockSpec((1, leaf_rows, tile), lambda j: (j // per_leaf, 0, j % per_leaf)),
+            pl.BlockSpec((cols, tile), lambda j: (0, j)),
             pl.BlockSpec((levels * width, tile), lambda j: (0, j)),
             pl.BlockSpec((1, width, cols), lambda j: (j // per_leaf, 0, 0)),
             pl.BlockSpec((steps * width, cols), lambda j: (0, 0)),
         ],
         out_specs=pl.BlockSpec((cols, tile), lambda j: (0, j)),
         compiler_params=pltpu.CompilerParams(vmem_limit_bytes=63 * MIB),
-    )(permuted, leaf_factor, basis, first, later)
+    )(field, basis, first, later)
 
 
 def solution(mesh):

time: 51.5 us -> 50.4 us (0.979)
  Pallas kernels: 51.4 us -> 50.2 us
    pallas_call x1, Pallas kernels: 8.32 us -> 6.07 us  [local(): pl.pallas_call(final_kernel, name='final_part', grid=(row_count // tile,)...]
    pallas_call x1, Pallas kernels: 43 us -> 44.1 us  [local(): pl.pallas_call(functools.partial(tree_kernel, levels, width), name='tree_...]
where the time goes in v2:
time: 50.4 us; the launch traced here: 50.2 us
  Pallas kernels  50.2 us (100%)
    pallas_call x1, Pallas kernels, local(): pl.pallas_call(functools.partial(tree_kernel, levels, width), name='tree_...  44.1 us
    pallas_call x1, Pallas kernels, local(): pl.pallas_call(final_kernel, name='final_part', grid=(row_count // tile,)...  6.07 us

profile of v2, /device:TPU:0, one launch (start us, length us, event | category | flops | bytes accessed | tf_op | source)
XLA Modules:
  0.0 50.2 jit_solution(11601322854418102696)
XLA Ops:
  0.0 44.1 %tree_part.1 = (f32[512,2048]{1,0:T(8,128)}, f32[2,64,512]{2,1,0:T(8,128)}, f32[192,512]{1,0:T(8,128)}) custom-call(s32[4,16]{1,0:T(4,128)} %ranks.1, bf16[512,2048]{1,0:T(8,128)(2,1)} %samples_hbm.1, s32[1,2048]{1,0:T(1,128)} %bitcast.4, bf16[256,2048]{1,0:T(8,128)(2,1)} %bitcast.2, f32[4,1,64,64]{3,2,1,0:T(8,128)} %coupling_hbm.1, ...), custom_call_target="tpu_custom_call" | custom-call | tf_op jit(solution)/shard_map/tree_part/pallas_call | solution.py:285
  44.1 6.1 %final_part.1 = f32[512,2048]{1,0:T(8,128)} custom-call(f32[512,2048]{1,0:T(8,128)} %get-tuple-element.8.field, bf16[256,2048]{1,0:T(8,128)(2,1)} %bitcast.3, f32[2,64,512]{2,1,0:T(8,128)} %get-tuple-element.9.first, f32[192,512]{1,0:T(8,128)} %get-tuple-element.10.later), custom_call_target="tpu_custom_call" | custom-call | tf_op jit(solution)/shard_map/final_part/pallas_call | solution.py:326
